TPU v7x, 32 devices: a whole 2x2x4 slice. The times are simulated.
32 devices in a mesh: expert: 8 (over z, y), half: 4 (over x, core).
Axes of the slice: x: 2, y: 2, z: 4, core: 2. Of those that a mesh axis runs over, the one named last changes fastest.
Arguments:
- tokens: bfloat16 [1024, 2048], P('expert', 'half'), may hold values from -6 to 6
- cotangent: bfloat16 [1024, 2048], P('expert', 'half'), may hold values from -4 to 4
- route: int32 [1024, 8], P('expert'), may hold values from 0 to 15, all different within a row; in each aligned block of 128 rows (0 to 127, 128 to 255, ...) at most 128 rows name the same one
- prob: bfloat16 [1024, 8], P('expert'), may hold values from 0.19921875 to 1
- w_gate: bfloat16 [16, 768, 2048], P('expert', 'half'), may hold values from -0.125 to 0.125
- w_up: bfloat16 [16, 768, 2048], P('expert', 'half'), may hold values from -0.125 to 0.125
- w_down: bfloat16 [16, 768, 2048], P('expert', 'half'), may hold values from -0.21875 to 0.21875
Outputs:
- grad_tokens: bfloat16 [1024, 2048], P('expert', 'half')
- grad_prob: float32 [1024, 8], P('expert')
- grad_gate: bfloat16 [16, 768, 2048], P('expert', 'half')
- grad_up: bfloat16 [16, 768, 2048], P('expert', 'half')
- grad_down: bfloat16 [16, 768, 2048], P('expert', 'half')
Inputs may be any that keep to these rules, and one draw needn't show every extreme that they name: `route`: each row names 8 different experts; among the rows of one device no expert is named more than 128 times, and that most is reached.
All inputs are finite; a program needn't handle non-finite values.
Results may differ from a plain program's by a relative error of at most 0.013.
Values may be sent and summed in bfloat16 or wider, within the bound.
A program may use at most 192 MiB of HBM per device.

v0:
```python
import functools

import jax
import jax.numpy as jnp
from jax import lax
from jax.experimental import pallas as pl
from jax.experimental.pallas import tpu as pltpu
from jax.sharding import PartitionSpec as P

BOTH = ("expert", "half")


def gather_all(block, groups, halves):
    rows, quarter = block.shape
    parts = lax.all_gather(block, BOTH, axis=0).reshape(groups, halves, rows, quarter)
    return parts.transpose(0, 2, 1, 3).reshape(groups * rows, halves * quarter)


LANES = 128
MESH = pl.DeviceIdType.MESH


def place(groups):
    e, h = lax.axis_index("expert"), lax.axis_index("half")
    return lax.div(e, 2), lax.rem(e, 2), lax.div(h, 2), lax.rem(h, 2)


def across(z, step):
    bit = 1
    while bit <= step:
        if step & bit:
            z = z + bit * (1 - 2 * lax.rem(lax.div(z, bit), 2))
        bit *= 2
    return z


def greet(peers):
    barrier = pltpu.get_barrier_semaphore()
    for peer in peers:
        pl.semaphore_signal(barrier, inc=1, device_id=peer, device_id_type=MESH)
    pl.semaphore_wait(barrier, len(peers))


def gather_kernel(
    groups, tok_ref, cot_ref, tab_ref, x_ref, d_ref, w_ref,
    send_sem, z_sem, p_sem, q_sem, c_sem, tab_send, tab_recv, own_sem,
):
    line = groups // 2
    z, y, x, c = place(groups)
    e, h = 2 * z + y, 2 * x + c
    rows, quarter = tok_ref.shape
    y_peer = (2 * z + 1 - y, h)
    x_peer = (e, 2 * (1 - x) + c)
    c_peer = (e, 2 * x + 1 - c)
    ring = [(lax.rem(e + s, groups), h) for s in range(1, groups)]
    greet(ring + [x_peer, c_peer])

    sends, owns = [], []

    def push(src, dst, peer, number, sem):
        copy = pltpu.make_async_remote_copy(
            src_ref=src, dst_ref=dst, send_sem=number, recv_sem=sem,
            device_id=peer, device_id_type=MESH,
        )
        copy.start()
        sends.append(copy)

    def slot(out, zz, yy, xx, cc):
        row = pl.multiple_of((2 * zz + yy) * rows, rows)
        col = pl.multiple_of((2 * xx + cc) * quarter, quarter)
        return out.at[pl.ds(row, rows), pl.ds(col, quarter)]

    arrays = []
    for a, (src, out) in enumerate(((tok_ref, x_ref), (cot_ref, d_ref))):
        first, second = (y_peer, x_peer) if a == 0 else (x_peer, y_peer)

        def at(step, kind, out=out, a=a):
            zz = across(z, step)
            flip_first, flip_second = kind % 2, kind // 2
            fy, fx = (flip_first, flip_second) if a == 0 else (flip_second, flip_first)
            return slot(out, zz, 1 - y if fy else y, 1 - x if fx else x, c)

        arrays.append((a, src, out, first, second, at))

    def wait(a, at, step, kind, sem):
        here = at(step, kind)
        pltpu.make_async_remote_copy(
            src_ref=here, dst_ref=here, send_sem=own_sem.at[a], recv_sem=sem,
            device_id=c_peer, device_id_type=MESH,
        ).wait_recv()

    for a, src, out, first, second, at in arrays:
        here = slot(out, z, y, x, c)
        for s in range(1, line):
            push(src, here, (2 * across(z, s) + y, h), send_sem.at[a, s - 1], z_sem.at[a, s])
        own = pltpu.make_async_copy(src, here, own_sem.at[a])
        own.start()
        owns.append(own)
    for s in range(1, groups):
        here = w_ref.at[pl.ds(pl.multiple_of(e * rows, rows), rows), :]
        push(tab_ref, here, ring[s - 1], tab_send.at[s], tab_recv.at[s])
    own = pltpu.make_async_copy(
        tab_ref, w_ref.at[pl.ds(pl.multiple_of(e * rows, rows), rows), :], own_sem.at[2]
    )
    own.start()
    owns.append(own)

    base = line - 1
    for s in range(line + 2):
        for a, src, out, first, second, at in arrays:
            if s < line:
                if s > 0:
                    wait(a, at, s, 0, z_sem.at[a, s])
                there = at(s, 0)
                have = src if s == 0 else there
                push(have, there, first, send_sem.at[a, base + s], p_sem.at[a, s])
                push(have, there, second, send_sem.at[a, base + line + s], q_sem.at[a, s])
                push(have, there, c_peer, send_sem.at[a, base + 3 * line + s], c_sem.at[a, s])
            if 1 <= s <= line:
                j = s - 1
                wait(a, at, j, 1, p_sem.at[a, j])
                there = at(j, 1)
                push(there, there, second, send_sem.at[a, base + 2 * line + j], q_sem.at[a, line + j])
                push(there, there, c_peer, send_sem.at[a, base + 4 * line + j], c_sem.at[a, line + j])
                wait(a, at, j, 2, q_sem.at[a, j])
                there = at(j, 2)
                push(there, there, c_peer, send_sem.at[a, base + 5 * line + j], c_sem.at[a, 2 * line + j])
            if s >= 2:
                j = s - 2
                wait(a, at, j, 3, q_sem.at[a, line + j])
                there = at(j, 3)
                push(there, there, c_peer, send_sem.at[a, base + 6 * line + j], c_sem.at[a, 3 * line + j])
    for s in range(1, groups):
        peer = lax.rem(e - s + groups, groups)
        here = w_ref.at[pl.ds(pl.multiple_of(peer * rows, rows), rows), :]
        pltpu.make_async_remote_copy(
            src_ref=here, dst_ref=here, send_sem=tab_send.at[s], recv_sem=tab_recv.at[s],
            device_id=c_peer, device_id_type=MESH,
        ).wait_recv()
    for a, src, out, first, second, at in arrays:
        for kind in range(4):
            for j in range(line):
                flips = (kind % 2, kind // 2) if a == 0 else (kind // 2, kind % 2)
                here = slot(
                    out, across(z, j),
                    1 - y if flips[0] else y, 1 - x if flips[1] else x, 1 - c,
                )
                pltpu.make_async_remote_copy(
                    src_ref=here, dst_ref=here, send_sem=own_sem.at[a],
                    recv_sem=c_sem.at[a, kind * line + j], device_id=c_peer, device_id_type=MESH,
                ).wait_recv()
    for own in owns:
        own.wait()
    for copy in sends:
        copy.wait_send()


def gather_fast(tokens, cotangent, table, groups, halves):
    rows, quarter = tokens.shape
    line = groups // 2
    padded = jnp.pad(table, ((0, 0), (0, -table.shape[1] % LANES)))
    full = jax.ShapeDtypeStruct((groups * rows, halves * quarter), tokens.dtype)
    dma = pltpu.SemaphoreType.DMA
    return pl.pallas_call(
        functools.partial(gather_kernel, groups),
        out_shape=(full, full, jax.ShapeDtypeStruct((groups * rows, padded.shape[1]), table.dtype)),
        in_specs=[pl.BlockSpec(memory_space=pltpu.VMEM)] * 3,
        out_specs=[pl.BlockSpec(memory_space=pl.ANY)] * 3,
        scratch_shapes=[
            dma((2, 8 * line)), dma((2, line)), dma((2, line)), dma((2, 2 * line)),
            dma((2, 4 * line)), dma((groups,)), dma((groups,)), dma((3,)),
        ],
        compiler_params=pltpu.CompilerParams(collective_id=0, has_side_effects=True),
    )(tokens, cotangent, padded)


def scatter_kernel(
    groups, halves, part, score, out_ref, back_ref, core, one_a, one_b, two_a, two_b, last,
    send_sem, recv_sem, score_send, score_recv, own_sem,
):
    line = groups // 2
    z, y, x, c = place(groups)
    e, h = 2 * z + y, 2 * x + c
    wide = out_ref.shape[1] // 2
    f32 = jnp.float32
    y_peer = (2 * z + 1 - y, h)
    x_peer = (e, 2 * (1 - x) + c)
    c_peer = (e, 2 * x + 1 - c)
    others = [(2 * lax.rem(z + s, line) + y, h) for s in range(1, line)]
    peers = [
        (lax.rem(e + i, groups), lax.rem(h + j, halves))
        for i in range(groups) for j in range(halves) if i + j
    ]
    greet(peers)

    def col(xx, cc, side):
        return pl.ds(pl.multiple_of((2 * xx + cc) * 2 * wide + side * wide, wide), wide)

    def push(src, dst, peer, number):
        copy = pltpu.make_async_remote_copy(
            src_ref=src, dst_ref=dst, send_sem=send_sem.at[number], recv_sem=recv_sem.at[number],
            device_id=peer, device_id_type=MESH,
        )
        copy.start()
        return copy

    def add(dst, src):
        dst[...] = (dst[...].astype(f32) + src[...].astype(f32)).astype(dst.dtype)

    copies = []
    order = ((0, 0), (1, 0), (1, 1), (0, 1))
    scores = []
    mine = e * halves + h

    def send_scores():
        for number, peer in enumerate(peers):
            copy = pltpu.make_async_remote_copy(
                src_ref=score.at[peer[0]], dst_ref=back_ref.at[mine],
                send_sem=score_send.at[number], recv_sem=score_recv.at[number],
                device_id=peer, device_id_type=MESH,
            )
            copy.start()
            scores.append(copy)

    own = pltpu.make_async_copy(score.at[e], back_ref.at[mine], own_sem.at[0])
    own.start()
    for number, (side, keep) in enumerate(order):
        xx = x if keep else 1 - x
        copies.append(
            push(part.at[:, :, :, col(xx, 1 - c, side)], core.at[side, keep], c_peer, number)
        )

    def settle(number):
        side, keep = order[number]
        copies[number].wait_recv()
        xx = x if keep else 1 - x

        @pl.loop(0, line)
        def _(i):
            for j in range(2):
                add(core.at[side, keep, i, j], part.at[i, j, :, col(xx, c, side)])

    settle(0)
    a1 = push(core.at[0, 0], one_a, x_peer, 4)
    settle(1)
    settle(2)
    b1 = push(core.at[1, :, :, 1 - y], one_b, y_peer, 5)
    send_scores()
    settle(3)
    a1.wait_recv()

    @pl.loop(0, line)
    def _(i):
        for j in range(2):
            add(one_a.at[i, j], core.at[0, 1, i, j])

    a2 = push(one_a.at[:, 1 - y], two_a, y_peer, 6)
    b1.wait_recv()

    @pl.loop(0, line)
    def _(i):
        for j in range(2):
            add(one_b.at[j, i], core.at[1, j, i, y])

    b2 = push(one_b.at[0], two_b, x_peer, 7)
    copies += [a1, b1, a2, b2]
    tails = ([], [])
    for side, copy, two in ((0, a2, two_a), (1, b2, two_b)):
        copy.wait_recv()

        @pl.loop(0, line)
        def _(i):
            add(two.at[i], one_a.at[i, y] if side == 0 else one_b.at[1, i])

        for s in range(1, line):
            number = 8 + side * line + s
            tails[side].append(
                push(two.at[lax.rem(z + s, line)], last.at[side, s - 1], others[s - 1], number)
            )
    for side, two in ((0, two_a), (1, two_b)):
        total = two[z].astype(f32)
        for s, copy in enumerate(tails[side]):
            copy.wait_recv()
            total = total + last[side, s].astype(f32)
        out_ref[:, side * wide:(side + 1) * wide] = total.astype(out_ref.dtype)
    for copy in scores:
        copy.wait_recv()
    own.wait()
    for copy in copies + tails[0] + tails[1] + scores:
        copy.wait_send()


def scatter_fast(part, score, groups, halves, rows, quarter):
    line = groups // 2
    wide = quarter // 2
    b16 = part.dtype
    dma = pltpu.SemaphoreType.DMA
    return pl.pallas_call(
        functools.partial(scatter_kernel, groups, halves),
        out_shape=(
            jax.ShapeDtypeStruct((rows, quarter), b16),
            jax.ShapeDtypeStruct((groups * halves,) + score.shape[1:], score.dtype),
        ),
        in_specs=[pl.BlockSpec(memory_space=pltpu.VMEM)] * 2,
        out_specs=[pl.BlockSpec(memory_space=pltpu.VMEM)] * 2,
        scratch_shapes=[
            pltpu.VMEM((2, 2, line, 2, rows, wide), b16),
            pltpu.VMEM((line, 2, rows, wide), b16),
            pltpu.VMEM((2, line, rows, wide), b16),
            pltpu.VMEM((line, rows, wide), b16),
            pltpu.VMEM((line, rows, wide), b16),
            pltpu.VMEM((2, line - 1, rows, wide), b16),
            dma((8 + 2 * line,)),
            dma((8 + 2 * line,)),
            dma((groups * halves - 1,)),
            dma((groups * halves - 1,)),
            dma((1,)),
        ],
        compiler_params=pltpu.CompilerParams(collective_id=1, has_side_effects=True),
    )(part.reshape(line, 2, rows, halves * quarter), score)


def per_device(tokens, cotangent, route, prob, w_gate, w_up, w_down):
    tok_rows, quarter = tokens.shape
    local_exp, units, width = w_gate.shape
    groups = lax.axis_size("expert")
    halves = lax.axis_size("half")
    experts = local_exp * groups
    total = groups * tok_rows
    f32 = jnp.float32
    me = lax.axis_index("expert")

    hit = route[:, :, None] == jnp.arange(experts, dtype=route.dtype)
    table = jnp.sum(jnp.where(hit, prob[:, :, None], 0).astype(f32), axis=1).astype(prob.dtype)
    fast = (
        groups > 2 and groups & (groups - 1) == 0 and halves == 2 * 2
        and tok_rows % LANES == 0 and quarter % (2 * LANES) == 0
        and total * width * 2 <= (1 << 23)
    )
    if fast:
        x, d, mine = gather_fast(tokens, cotangent, table, groups, halves)
        mine = lax.dynamic_slice_in_dim(mine, me * local_exp, local_exp, axis=1)
    else:
        mine = lax.all_to_all(
            table.reshape(tok_rows, groups, local_exp), "expert",
            split_axis=1, concat_axis=0, tiled=True,
        ).reshape(total, local_exp)
        x = gather_all(tokens, groups, halves)
        d = gather_all(cotangent, groups, halves)
    weight = jnp.repeat(mine.astype(f32), units, axis=1)

    wg = w_gate.reshape(local_exp * units, width)
    wu = w_up.reshape(local_exp * units, width)
    wd = w_down.reshape(local_exp * units, width)
    nt = (((1,), (1,)), ((), ()))
    tn = (((0,), (0,)), ((), ()))
    gate = lax.dot_general(x, wg, nt, preferred_element_type=f32)
    upval = lax.dot_general(x, wu, nt, preferred_element_type=f32)
    raw = lax.dot_general(d, wd, nt, preferred_element_type=f32)
    sig = jax.nn.sigmoid(gate)
    act = gate * sig
    hidden = act * upval
    score = jnp.sum((hidden * raw).reshape(total, local_exp, units), axis=2)
    dact = weight * raw
    hp = (weight * hidden).astype(jnp.bfloat16)
    dgate = (dact * upval * sig * (1.0 + gate * (1.0 - sig))).astype(jnp.bfloat16)
    dup = (dact * act).astype(jnp.bfloat16)
    part = lax.dot_general(
        jnp.concatenate([dgate, dup], axis=1), jnp.concatenate([wg, wu], axis=0),
        (((1,), (0,)), ((), ())), preferred_element_type=f32,
    ).astype(jnp.bfloat16)
    if fast:
        by_group = score.reshape(groups, tok_rows, local_exp).transpose(0, 2, 1)
        by_group = jnp.pad(by_group, ((0, 0), (0, -local_exp % 8), (0, 0)))
        grad_tokens, back = scatter_fast(part, by_group, groups, halves, tok_rows, quarter)
        back = back[:, :local_exp].reshape(groups, halves, local_exp, tok_rows)
        back = jnp.sum(back, axis=1).transpose(2, 0, 1).reshape(tok_rows, 1, experts)
    else:
        part = part.reshape(groups, tok_rows, halves, quarter).transpose(0, 2, 1, 3)
        grad_tokens = lax.psum_scatter(
            part.reshape(groups * halves * tok_rows, quarter), BOTH,
            scatter_dimension=0, tiled=True,
        )
        sent = jnp.broadcast_to(
            score.reshape(groups, 1, tok_rows, local_exp), (groups, halves, tok_rows, local_exp)
        ).reshape(groups * halves, tok_rows * local_exp)
        back = lax.all_to_all(sent, BOTH, split_axis=0, concat_axis=0, tiled=True)
        back = jnp.sum(back.reshape(groups, halves, tok_rows, local_exp), axis=1)
        back = back.transpose(1, 0, 2).reshape(tok_rows, 1, experts)
    grad_prob = jnp.sum(jnp.where(hit, back, 0), axis=2)
    shape = (local_exp, units, width)
    grad_gate = lax.dot_general(dgate, x, tn, preferred_element_type=f32).astype(jnp.bfloat16)
    grad_up = lax.dot_general(dup, x, tn, preferred_element_type=f32).astype(jnp.bfloat16)
    grad_down = lax.dot_general(hp, d, tn, preferred_element_type=f32).astype(jnp.bfloat16)
    return (
        grad_tokens,
        grad_prob,
        grad_gate.reshape(shape),
        grad_up.reshape(shape),
        grad_down.reshape(shape),
    )


def solution(mesh):
    in_specs = (
        P("expert", "half"),
        P("expert", "half"),
        P("expert", None),
        P("expert", None),
        P("expert", "half", None),
        P("expert", "half", None),
        P("expert", "half", None),
    )
    out_specs = (
        P("expert", "half"),
        P("expert", None),
        P("expert", "half", None),
        P("expert", "half", None),
        P("expert", "half", None),
    )
    return jax.shard_map(
        per_device, mesh=mesh, in_specs=in_specs, out_specs=out_specs, check_vma=False
    )
```

profile of v0, /device:TPU:0, one launch (start us, length us, event | category | flops | bytes accessed | tf_op | source)
XLA Modules:
  0.0 130.5 jit_solution(11569218448676985583)
XLA Ops:
  0.6 0.0 copy-start
  0.7 1.4 %copy-done = bf16[2,192,2048]{2,1,0:T(8,128)(2,1)S(1)} copy-done((bf16[2,192,2048]{2,1,0:T(8,128)(2,1)S(1)}, bf16[2,192,2048]{2,1,0:T(8,128)(2,1)}, u32[]{:S(2)}) %copy-start) | copy-done | bytes 1572888
  2.0 0.7 fusion.9
  2.8 0.1 copy.23
  2.9 0.6 pad.8.tab_ref
  3.5 51.6 %shard_map.110 = (bf16[1024,2048]{1,0:T(8,128)(2,1)}, bf16[1024,2048]{1,0:T(8,128)(2,1)}, bf16[1024,128]{1,0:T(8,128)(2,1)}) custom-call(bf16[128,512]{1,0:T(8,128)(2,1)} %tok_ref.1, bf16[128,512]{1,0:T(8,128)(2,1)} %cot_ref.1, bf16[128,128]{1,0:T(8,128)(2,1)} %pad.8.tab_ref), custom_call_target="tpu_custom_call" | custom-call | tf_op jit(solution)/shard_map/pallas_call | solution.py:164
  55.1 1.1 dynamic-slice_convert_fusion
  56.2 0.2 copy.24
  56.4 0.0 copy-start.5
  56.4 0.0 copy-start.7
  56.4 4.7 %fusion.12 = f32[1024,384]{0,1:T(8,128)S(1)} fusion(bf16[1024,2048]{1,0:T(8,128)(2,1)} %get-tuple-element.12, bf16[384,2048]{1,0:T(8,128)(2,1)} %bitcast.44), kind=kOutput, calls=%fused_computation.26 | convolution fusion | flops 1610612736 | bytes 7340032 | tf_op jit(solution)/shard_map/dot_general | solution.py:357
  61.0 0.0 copy-done.5
  61.1 0.0 copy-done.7
  61.1 0.0 copy-start.1
  61.1 1.8 %fusion.11 = f32[1024,384]{0,1:T(8,128)S(1)} fusion(bf16[1024,2048]{1,0:T(8,128)(2,1)S(1)} %copy-done.5, bf16[384,2048]{1,0:T(8,128)(2,1)S(1)} %bitcast.42), kind=kOutput, calls=%fused_computation.25 | convolution fusion | flops 1610612736 | bytes 7340032 | tf_op jit(solution)/shard_map/dot_general | solution.py:358
  62.9 0.3 copy-done.1
  63.3 3.7 %multiply_multiply_fusion = (f32[1024,384]{0,1:T(8,128)S(1)}, bf16[1024,384]{0,1:T(8,128)(2,1)}, bf16[1024,384]{0,1:T(8,128)(2,1)S(1)}, bf16[1024,384]{0,1:T(8,128)(2,1)}) fusion(f32[1024,384]{0,1:T(8,128)S(1)} %fusion.11, f32[1024,384]{0,1:T(8,128)S(1)} %fusion.12, f32[1024,2]{0,1:T(2,128)S(1)} %copy.24, bf16[1024,2048]{1,0:T(8,128)(2,1)S(1)} %copy-done.1, ...), kind=kOutput, calls=%fused_computation.17 | convolution fusion | flops 1617690624 | bytes 12853248 | tf_op jit(solution)/shard_map/dot_general | solution.py:359
  66.9 3.0 %convolution_convert_fusion.1 = bf16[384,2048]{1,0:T(8,128)(2,1)} fusion(bf16[1024,384]{0,1:T(8,128)(2,1)S(1)} %get-tuple-element.17, bf16[1024,2048]{1,0:T(8,128)(2,1)S(1)} %copy-done.1), kind=kOutput, calls=%fused_computation.4 | convolution fusion | flops 1611399168 | bytes 6553600 | tf_op jit(solution)/shard_map/dot_general | solution.py:394
  69.9 0.1 reduce_sum.40
  70.0 0.6 pad.9.score
  70.6 0.0 copy-start.3
  70.6 0.0 copy-start.6
  70.6 5.5 %convolution_convert_fusion.3 = bf16[384,2048]{1,0:T(8,128)(2,1)} fusion(bf16[1024,384]{0,1:T(8,128)(2,1)} %get-tuple-element.16, bf16[1024,2048]{1,0:T(8,128)(2,1)} %get-tuple-element.12), kind=kOutput, calls=%fused_computation.6 | convolution fusion | flops 1611399168 | bytes 6553600 | tf_op jit(solution)/shard_map/dot_general | solution.py:392
  76.1 0.0 copy-done.3
  76.2 0.0 copy-done.6
  76.2 0.0 copy-start.2
  76.2 0.0 copy-start.8
  76.2 0.0 copy-start.9
  76.2 3.0 %convolution_convert_fusion.2 = bf16[384,2048]{1,0:T(8,128)(2,1)} fusion(bf16[1024,384]{0,1:T(8,128)(2,1)S(1)} %copy-done.3, bf16[1024,2048]{1,0:T(8,128)(2,1)S(1)} %copy-done.6), kind=kOutput, calls=%fused_computation.5 | convolution fusion | flops 1611399168 | bytes 6553600 | tf_op jit(solution)/shard_map/dot_general | solution.py:393
  79.2 0.0 copy-done.2
  79.2 0.0 copy-done.8
  79.2 0.0 copy-done.9
  79.2 5.3 %convolution_convert_fusion = bf16[1024,2048]{1,0:T(8,128)(2,1)} fusion(bf16[384,2048]{1,0:T(8,128)(2,1)S(1)} %bitcast.43, bf16[384,2048]{1,0:T(8,128)(2,1)S(1)} %bitcast.45, bf16[1024,384]{0,1:T(8,128)(2,1)S(1)} %copy-done.3, bf16[1024,384]{0,1:T(8,128)(2,1)S(1)} %copy-done.2), kind=kOutput, calls=%fused_computation | convolution fusion | flops 3232759808 | bytes 8912896 | tf_op jit(solution)/shard_map/dot_general | solution.py:368
  84.4 0.0 copy-start.4
  84.4 43.0 %shard_map.111 = (bf16[128,512]{1,0:T(8,128)(2,1)}, f32[32,8,128]{2,1,0:T(8,128)}) custom-call(bf16[4,2,128,2048]{3,2,1,0:T(8,128)(2,1)} %bitcast.39, f32[8,8,128]{2,1,0:T(8,128)} %pad.9.score), custom_call_target="tpu_custom_call" | custom-call | tf_op jit(solution)/shard_map/pallas_call | solution.py:298
  127.4 0.9 bitcast_reduce_fusion
  128.4 0.0 copy-done.4
  128.4 0.6 select_reduce_fusion
  129.0 1.6 %copy.27 = bf16[128,512]{1,0:T(8,128)(2,1)} copy(bf16[128,512]{1,0:T(8,128)(2,1)} %get-tuple-element.24) | data formatting | bytes 262144
Async XLA Ops:
  0.6 1.4 %copy-start = (bf16[2,192,2048]{2,1,0:T(8,128)(2,1)S(1)}, bf16[2,192,2048]{2,1,0:T(8,128)(2,1)}, u32[]{:S(2)}) copy-start(bf16[2,192,2048]{2,1,0:T(8,128)(2,1)} %param.13) | copy-start | bytes 4718596
  56.4 4.7 %copy-start.5 = (bf16[1024,2048]{1,0:T(8,128)(2,1)S(1)}, bf16[1024,2048]{1,0:T(8,128)(2,1)}, u32[]{:S(2)}) copy-start(bf16[1024,2048]{1,0:T(8,128)(2,1)} %get-tuple-element.12) | copy-start | bytes 12582916
  56.4 4.7 %copy-start.7 = (bf16[2,192,2048]{2,1,0:T(8,128)(2,1)S(1)}, bf16[2,192,2048]{2,1,0:T(8,128)(2,1)}, u32[]{:S(2)}) copy-start(bf16[2,192,2048]{2,1,0:T(8,128)(2,1)} %param.12) | copy-start | bytes 4718596
  61.1 2.2 %copy-start.1 = (bf16[1024,2048]{1,0:T(8,128)(2,1)S(1)}, bf16[1024,2048]{1,0:T(8,128)(2,1)}, u32[]{:S(2)}) copy-start(bf16[1024,2048]{1,0:T(8,128)(2,1)} %get-tuple-element.11) | copy-start | bytes 12582916
  70.6 5.5 %copy-start.3 = (bf16[1024,384]{0,1:T(8,128)(2,1)S(1)}, bf16[1024,384]{0,1:T(8,128)(2,1)}, u32[]{:S(2)}) copy-start(bf16[1024,384]{0,1:T(8,128)(2,1)} %get-tuple-element.18) | copy-start | bytes 2359300
  70.6 5.5 %copy-start.6 = (bf16[1024,2048]{1,0:T(8,128)(2,1)S(1)}, bf16[1024,2048]{1,0:T(8,128)(2,1)}, u32[]{:S(2)}) copy-start(bf16[1024,2048]{1,0:T(8,128)(2,1)} %get-tuple-element.12) | copy-start | bytes 12582916
  76.2 3.0 %copy-start.2 = (bf16[1024,384]{0,1:T(8,128)(2,1)S(1)}, bf16[1024,384]{0,1:T(8,128)(2,1)}, u32[]{:S(2)}) copy-start(bf16[1024,384]{0,1:T(8,128)(2,1)} %get-tuple-element.16) | copy-start | bytes 2359300
  76.2 3.0 %copy-start.8 = (bf16[2,192,2048]{2,1,0:T(8,128)(2,1)S(1)}, bf16[2,192,2048]{2,1,0:T(8,128)(2,1)}, u32[]{:S(2)}) copy-start(bf16[2,192,2048]{2,1,0:T(8,128)(2,1)} %param.12) | copy-start | bytes 4718596
  76.2 3.0 %copy-start.9 = (bf16[2,192,2048]{2,1,0:T(8,128)(2,1)S(1)}, bf16[2,192,2048]{2,1,0:T(8,128)(2,1)}, u32[]{:S(2)}) copy-start(bf16[2,192,2048]{2,1,0:T(8,128)(2,1)} %param.11) | copy-start | bytes 4718596
  84.4 43.9 %copy-start.4 = (s32[128,8]{0,1:T(8,128)S(1)}, s32[128,8]{0,1:T(8,128)}, u32[]{:S(2)}) copy-start(s32[128,8]{0,1:T(8,128)} %param.9) | copy-start | bytes 12292
where the time goes:
time: 131 us
  Pallas kernels  94.6 us (72%)
  matrix products  26.9 us (21%)
  local copies, waits for them, and re-layouts  4.9 us (4%)
  other arithmetic  3.44 us (3%)
    pallas_call x1, Pallas kernels, gather_fast(): pl.pallas_call(functools.partial(gather_kernel, groups), out_shape=(full,...  51.6 us
    pallas_call x1, Pallas kernels, scatter_fast(): pl.pallas_call(functools.partial(scatter_kernel, groups, halves), out_sha...  43 us
    dot_general x1, matrix products, per_device(): lax.dot_general(dgate, x, tn, preferred_element_type=f32)  5.51 us
    dot_general x1, matrix products, per_device(): lax.dot_general(jnp.concatenate([dgate, dup], axis=1), jnp.concatenate([w...  5.27 us
    dot_general x1, matrix products, per_device(): gate = lax.dot_general(x, wg, nt, preferred_element_type=f32)  4.65 us
    dot_general x1, matrix products, per_device(): raw = lax.dot_general(d, wd, nt, preferred_element_type=f32)  3.69 us
    unnamed x21, local copies, waits for them, and re-layouts  3.35 us
    dot_general x1, matrix products, per_device(): lax.dot_general(dup, x, tn, preferred_element_type=f32).astype(jnp.bfloat16)  2.97 us

commit v1 on v0

v1 whole, which is shorter than its diff:
```python
import functools

import jax
import jax.numpy as jnp
from jax import lax
from jax.experimental import pallas as pl
from jax.experimental.pallas import tpu as pltpu
from jax.sharding import PartitionSpec as P

BOTH = ("expert", "half")


def gather_all(block, groups, halves):
    rows, quarter = block.shape
    parts = lax.all_gather(block, BOTH, axis=0).reshape(groups, halves, rows, quarter)
    return parts.transpose(0, 2, 1, 3).reshape(groups * rows, halves * quarter)


LANES = 128
VMEM_BYTES = 48 << 20
MESH = pl.DeviceIdType.MESH


def place(groups):
    e, h = lax.axis_index("expert"), lax.axis_index("half")
    return lax.div(e, 2), lax.rem(e, 2), lax.div(h, 2), lax.rem(h, 2)


def across(z, step):
    bit = 1
    while bit <= step:
        if step & bit:
            z = z + bit * (1 - 2 * lax.rem(lax.div(z, bit), 2))
        bit *= 2
    return z


def greet(peers):
    barrier = pltpu.get_barrier_semaphore()
    for peer in peers:
        pl.semaphore_signal(barrier, inc=1, device_id=peer, device_id_type=MESH)
    pl.semaphore_wait(barrier, len(peers))


def fused_kernel(
    groups, halves, local_exp, tok_ref, cot_ref, route_ref, prob_ref, wg_ref, wu_ref, wd_ref,
    gt_ref, gp_ref, gg_ref, gu_ref, gd_ref,
    xb, db, wgu, wdn, gates, raws, dgu, hps, turned, tab_own, tab_in, score, back,
    psend, own, cin, acc, xin0, yin0, yin1, xin1, t0, t1, fin, zin,
    first_send, second_send, core_send, z_send, z_sem, p_sem, q_sem, c_sem, own_sem, w_sem,
    tab_send, tab_recv, score_send, score_recv,
    part_send, part_recv, hop_send, hop_recv, last_send, last_recv,
):
    line = groups // 2
    z, y, x, c = place(groups)
    e, h = 2 * z + y, 2 * x + c
    rows, quarter = tok_ref.shape
    wide = quarter // 2
    hidden_rows, width = wg_ref.shape
    units = hidden_rows // local_exp
    experts = local_exp * groups
    top = route_ref.shape[1]
    f32, b16 = jnp.float32, tok_ref.dtype
    nt = (((1,), (1,)), ((), ()))
    nn = (((1,), (0,)), ((), ()))
    y_peer = (2 * z + 1 - y, h)
    x_peer = (e, 2 * (1 - x) + c)
    c_peer = (e, 2 * x + 1 - c)

    eye = (
        lax.broadcasted_iota(jnp.int32, (top, top), 0)
        == lax.broadcasted_iota(jnp.int32, (top, top), 1)
    ).astype(f32)
    flip = lambda a: lax.dot_general(eye, a, nt, preferred_element_type=f32)
    route_t = flip(route_ref[...].astype(f32))
    prob_t = flip(prob_ref[...].astype(f32))
    row_of = lax.broadcasted_iota(jnp.int32, (experts, rows), 0).astype(f32)
    table = jnp.zeros((experts, rows), f32)
    for k in range(top):
        table = table + jnp.where(row_of == route_t[k:k + 1, :], prob_t[k:k + 1, :], 0.0)
    tab_own[...] = table
    tab_in[0, 0] = table

    greet([
        (lax.rem(e + i, groups), lax.rem(h + j, halves))
        for i in range(groups) for j in range(halves) if i + j
    ])
    sends, owns = [], []

    def push(src, dst, peer, number, sem):
        copy = pltpu.make_async_remote_copy(
            src_ref=src, dst_ref=dst, send_sem=number, recv_sem=sem,
            device_id=peer, device_id_type=MESH,
        )
        copy.start()
        sends.append(copy)
        return copy

    def arrived(dst, sem):
        pltpu.make_async_remote_copy(
            src_ref=dst, dst_ref=dst, send_sem=own_sem.at[0], recv_sem=sem,
            device_id=c_peer, device_id_type=MESH,
        ).wait_recv()

    def local(src, dst, sem):
        copy = pltpu.make_async_copy(src, dst, sem)
        copy.start()
        return copy

    def slot(out, s, yy, xx, cc):
        row = pl.multiple_of((2 * s + yy) * rows, rows)
        col = pl.multiple_of((2 * xx + cc) * quarter, quarter)
        return out.at[pl.ds(row, rows), pl.ds(col, quarter)]

    pair = ((tok_ref, xb), (cot_ref, db))

    def at(a, s, kind, cc):
        along = (kind % 2, kind // 2) if a == 0 else (kind // 2, kind % 2)
        return slot(pair[a][1], s, 1 - y if along[0] else y, 1 - x if along[1] else x, cc)

    hops = ((y_peer, x_peer), (x_peer, y_peer))

    def gather_own(s):
        have = []
        for a in range(2):
            there = at(a, s, 0, c)
            if s > 0:
                arrived(there, z_sem.at[a, s])
            have.append((pair[a][0] if s == 0 else there, there))
            push(*have[a], hops[a][0], first_send.at[a, s], p_sem.at[a, s])
        for a in range(2):
            push(*have[a], hops[a][1], second_send.at[a, s], q_sem.at[a, s])
        for a in range(2):
            push(*have[a], c_peer, core_send.at[a, s], c_sem.at[a, s])

    def gather_first(s):
        for a in range(2):
            there = at(a, s, 1, c)
            arrived(there, p_sem.at[a, s])
            push(there, there, hops[a][1], second_send.at[a, line + s], q_sem.at[a, line + s])
        for a in range(2):
            there = at(a, s, 1, c)
            push(there, there, c_peer, core_send.at[a, line + s], c_sem.at[a, line + s])

    def gather_second(s, kind):
        for a in range(2):
            there = at(a, s, kind, c)
            arrived(there, q_sem.at[a, (kind - 2) * line + s])
            push(there, there, c_peer, core_send.at[a, kind * line + s], c_sem.at[a, kind * line + s])

    def gather_core(s):
        for a in range(2):
            for kind in range(4):
                arrived(at(a, s, kind, 1 - c), c_sem.at[a, kind * line + s])

    def plane(s):
        return pl.ds(2 * s * rows, 2 * rows)

    def forward(s):
        gates[...] = lax.dot_general(wgu[...], xb[plane(s), :], nt, preferred_element_type=f32)

    def middle(s):
        raws[...] = lax.dot_general(wdn[...], db[plane(s), :], nt, preferred_element_type=f32)
        chunk = 32 if units % 32 == 0 else 16
        expert_of = lax.broadcasted_iota(jnp.int32, (experts, rows), 0)
        lane = pl.ds(2 * s * rows, 2 * rows)
        sums = []
        tabs = [tab_in[s, y], tab_in[s, 1 - y]]
        for l in range(local_exp):
            weight = jnp.concatenate([
                jnp.sum(jnp.where(expert_of == local_exp * e + l, t, 0.0), axis=0, keepdims=True)
                for t in tabs
            ], axis=1)

            def step(i, total, l=l, weight=weight):
                at_row = pl.multiple_of(l * units + i * chunk, chunk)
                up_row = pl.multiple_of(hidden_rows + l * units + i * chunk, chunk)
                g = gates[pl.ds(at_row, chunk), :]
                u = gates[pl.ds(up_row, chunk), :]
                r = raws[pl.ds(at_row, chunk), :]
                sig = jax.nn.sigmoid(g)
                act = g * sig
                hidden = act * u
                dact = weight * r
                hps[pl.ds(at_row, chunk), lane] = (weight * hidden).astype(b16)
                dgu[pl.ds(at_row, chunk), lane] = (
                    dact * u * sig * (1.0 + g * (1.0 - sig))
                ).astype(b16)
                dgu[pl.ds(up_row, chunk), lane] = (dact * act).astype(b16)
                return total + jnp.sum((hidden * r).reshape(chunk // 8, 8, 2 * rows), axis=0)

            total = lax.fori_loop(0, units // chunk, step, jnp.zeros((8, 2 * rows), f32))
            sums.append(jnp.sum(total, axis=0, keepdims=True))
        sub = lax.broadcasted_iota(jnp.int32, (8, rows), 0)
        for yy in range(2):
            block = jnp.zeros((8, rows), f32)
            for l in range(local_exp):
                block = jnp.where(sub == l, sums[l][:, yy * rows:(yy + 1) * rows], block)
            score[s, yy] = block
        turned[...] = dgu[:, lane].T

    def part_of(xx, cc):
        cols = pl.ds(pl.multiple_of((2 * xx + cc) * quarter, quarter), quarter)
        return lax.dot_general(turned[...], wgu[:, cols], nn, preferred_element_type=f32).astype(b16)

    def send_part(s):
        copies = []
        for xx in range(2):
            psend[s, xx] = part_of(xx, 1 - c)
        for xx in range(2):
            push(psend.at[s, xx], cin.at[s, xx], c_peer, part_send.at[s, xx], part_recv.at[s, xx])
        for xx in range(2):
            own[s, xx] = part_of(xx, c)

    def flipped(dy):
        return 1 - y if dy else y

    def send_score(s):
        for dy in range(2):
            for j in range(halves):
                if s + dy + j == 0:
                    owns.append(local(score.at[0, y], back.at[0, 0, h], own_sem.at[3]))
                    continue
                push(
                    score.at[s, flipped(dy)], back.at[s, dy, h],
                    (2 * across(z, s) + flipped(dy), lax.rem(h + j, halves)),
                    score_send.at[s, dy, j], score_recv.at[s, dy, j],
                )

    step_rows = 32

    def row_loop(count):
        return pl.loop(0, count // step_rows)

    def some(i):
        return pl.ds(pl.multiple_of(i * step_rows, step_rows), step_rows)

    def settle_core(s):
        for xx in range(2):
            arrived(cin.at[s, xx], part_recv.at[s, xx])

            @row_loop(2 * rows)
            def _(i):
                both = own[s, xx, some(i)].astype(f32) + cin[s, xx, some(i)].astype(f32)
                acc[s, 0, xx, some(i)] = both[:, :wide].astype(b16)
                acc[s, 1, xx, some(i)] = both[:, wide:].astype(b16)

        push(acc.at[s, 0, 1 - x], xin0.at[s], x_peer, hop_send.at[s, 0], hop_recv.at[s, 0])
        away = pl.ds(pl.multiple_of((1 - y) * rows, rows), rows)
        push(acc.at[s, 1, :, away], yin1.at[s], y_peer, hop_send.at[s, 1], hop_recv.at[s, 1])

    def settle_first(s):
        arrived(xin0.at[s], hop_recv.at[s, 0])

        @row_loop(2 * rows)
        def _(i):
            t0[s, some(i)] = (
                acc[s, 0, x, some(i)].astype(f32) + xin0[s, some(i)].astype(f32)
            ).astype(b16)

        away = pl.ds(pl.multiple_of((1 - y) * rows, rows), rows)
        push(t0.at[s, away], yin0.at[s], y_peer, hop_send.at[s, 2], hop_recv.at[s, 2])
        arrived(yin1.at[s], hop_recv.at[s, 1])

        @row_loop(rows)
        def _(i):
            here = pl.ds(pl.multiple_of(y * rows + i * step_rows, step_rows), step_rows)
            for xx in range(2):
                t1[s, xx, some(i)] = (
                    acc[s, 1, xx, here].astype(f32) + yin1[s, xx, some(i)].astype(f32)
                ).astype(b16)

        push(t1.at[s, 1 - x], xin1.at[s], x_peer, hop_send.at[s, 3], hop_recv.at[s, 3])

    def settle_second(s):
        arrived(yin0.at[s], hop_recv.at[s, 2])
        arrived(xin1.at[s], hop_recv.at[s, 3])

        @row_loop(rows)
        def _(i):
            here = pl.ds(pl.multiple_of(y * rows + i * step_rows, step_rows), step_rows)
            fin[s, some(i), :wide] = (
                t0[s, here].astype(f32) + yin0[s, some(i)].astype(f32)
            ).astype(b16)
            fin[s, some(i), wide:] = (
                t1[s, x, some(i)].astype(f32) + xin1[s, some(i)].astype(f32)
            ).astype(b16)

        if s > 0:
            push(fin.at[s], zin.at[s], (2 * across(z, s) + y, h), last_send.at[s], last_recv.at[s])

    cut = quarter

    def grads_in(n):
        cols = pl.ds(n * cut, cut)
        both = lax.dot_general(dgu[...], xb[:, cols], nn, preferred_element_type=f32).astype(b16)
        gg_ref[:, cols] = both[:hidden_rows]
        gu_ref[:, cols] = both[hidden_rows:]

    def grads_out(n):
        cols = pl.ds(n * cut, cut)
        gd_ref[:, cols] = lax.dot_general(
            hps[...], db[:, cols], nn, preferred_element_type=f32
        ).astype(b16)

    gather_own(0)
    for a in range(2):
        for s in range(1, line):
            push(
                pair[a][0], slot(pair[a][1], s, y, x, c), (2 * across(z, s) + y, h),
                z_send.at[a, s], z_sem.at[a, s],
            )
    weights = [
        local(wg_ref, wgu.at[pl.ds(0, hidden_rows)], w_sem.at[0]),
        local(wu_ref, wgu.at[pl.ds(hidden_rows, hidden_rows)], w_sem.at[1]),
        local(wd_ref, wdn, w_sem.at[2]),
    ]
    mine = [local(pair[a][0], at(a, 0, 0, c), own_sem.at[1 + a]) for a in range(2)]
    for s in range(line):
        for dy in range(2):
            if s + dy:
                push(
                    tab_own, tab_in.at[s, dy], (2 * across(z, s) + flipped(dy), h),
                    tab_send.at[s, dy], tab_recv.at[s, dy],
                )
    gather_first(0)
    for copy in weights + mine:
        copy.wait()

    for s in range(line):
        if s + 1 < line:
            gather_own(s + 1)
        if s >= 1:
            settle_core(s - 1)
        gather_second(s, 2)
        gather_second(s, 3)
        gather_core(s)
        for dy in range(2):
            if s + dy:
                arrived(tab_in.at[s, dy], tab_recv.at[s, dy])
        if s >= 2:
            settle_second(s - 2)
        forward(s)
        if s + 1 < line:
            gather_first(s + 1)
        if s >= 1:
            settle_first(s - 1)
        middle(s)
        send_part(s)
        send_score(s)

    settle_core(line - 1)
    settle_second(line - 2)
    pieces = width // cut
    halfway = pieces // 2
    for n in range(halfway):
        grads_in(n)
    settle_first(line - 1)
    for n in range(halfway, pieces):
        grads_in(n)
    settle_second(line - 1)
    for n in range(pieces):
        grads_out(n)

    for copy in owns:
        copy.wait()
    for s in range(line):
        for dy in range(2):
            for j in range(halves):
                if s + dy + j:
                    arrived(
                        back.at[s, dy, lax.rem(h + halves - j, halves)], score_recv.at[s, dy, j]
                    )
    total = jnp.zeros((top, rows), f32)
    for s in range(line):
        for dy in range(2):
            block = back[s, dy, 0]
            for j in range(1, halves):
                block = block + back[s, dy, j]
            first = local_exp * (2 * across(z, s) + flipped(dy))
            for l in range(local_exp):
                total = total + jnp.where(
                    route_t == (first + l).astype(f32), block[l:l + 1, :], 0.0
                )
    gp_ref[...] = total
    for s in range(1, line):
        arrived(zin.at[s], last_recv.at[s])

    @row_loop(rows)
    def _(i):
        whole = fin[0, some(i)].astype(f32)
        for s in range(1, line):
            whole = whole + zin[s, some(i)].astype(f32)
        gt_ref[some(i)] = whole.astype(b16)

    for copy in sends:
        copy.wait_send()


def fused(tokens, cotangent, route, prob, wg, wu, wd, groups, halves, local_exp):
    rows, quarter = tokens.shape
    line, wide = groups // 2, quarter // 2
    hidden_rows, width = wg.shape
    experts, top = local_exp * groups, route.shape[1]
    b16, f32 = tokens.dtype, jnp.float32
    dma = pltpu.SemaphoreType.DMA
    vmem = pl.BlockSpec(memory_space=pltpu.VMEM)
    hbm = pl.BlockSpec(memory_space=pl.ANY)
    total = groups * rows
    grad = jax.ShapeDtypeStruct((hidden_rows, width), b16)
    return pl.pallas_call(
        functools.partial(fused_kernel, groups, halves, local_exp),
        out_shape=(
            jax.ShapeDtypeStruct((rows, quarter), b16),
            jax.ShapeDtypeStruct((top, rows), f32),
            grad, grad, grad,
        ),
        in_specs=[vmem] * 4 + [hbm] * 3,
        out_specs=[vmem] * 5,
        scratch_shapes=[
            pltpu.VMEM((total, width), b16),
            pltpu.VMEM((total, width), b16),
            pltpu.VMEM((2 * hidden_rows, width), b16),
            pltpu.VMEM((hidden_rows, width), b16),
            pltpu.VMEM((2 * hidden_rows, 2 * rows), f32),
            pltpu.VMEM((hidden_rows, 2 * rows), f32),
            pltpu.VMEM((2 * hidden_rows, total), b16),
            pltpu.VMEM((hidden_rows, total), b16),
            pltpu.VMEM((2 * rows, 2 * hidden_rows), b16),
            pltpu.VMEM((experts, rows), f32),
            pltpu.VMEM((line, 2, experts, rows), f32),
            pltpu.VMEM((line, 2, 8, rows), f32),
            pltpu.VMEM((line, 2, halves, 8, rows), f32),
            pltpu.VMEM((line, 2, 2 * rows, quarter), b16),
            pltpu.VMEM((line, 2, 2 * rows, quarter), b16),
            pltpu.VMEM((line, 2, 2 * rows, quarter), b16),
            pltpu.VMEM((line, 2, 2, 2 * rows, wide), b16),
            pltpu.VMEM((line, 2 * rows, wide), b16),
            pltpu.VMEM((line, rows, wide), b16),
            pltpu.VMEM((line, 2, rows, wide), b16),
            pltpu.VMEM((line, rows, wide), b16),
            pltpu.VMEM((line, 2 * rows, wide), b16),
            pltpu.VMEM((line, 2, rows, wide), b16),
            pltpu.VMEM((line, rows, quarter), b16),
            pltpu.VMEM((line, rows, quarter), b16),
            dma((2, line)), dma((2, 2 * line)), dma((2, 4 * line)), dma((2, line)),
            dma((2, line)), dma((2, line)), dma((2, 2 * line)), dma((2, 4 * line)),
            dma((4,)), dma((3,)),
            dma((line, 2)), dma((line, 2)),
            dma((line, 2, halves)), dma((line, 2, halves)),
            dma((line, 2)), dma((line, 2)),
            dma((line, 4)), dma((line, 4)),
            dma((line,)), dma((line,)),
        ],
        compiler_params=pltpu.CompilerParams(
            collective_id=0, has_side_effects=True, vmem_limit_bytes=VMEM_BYTES
        ),
    )(tokens, cotangent, route, prob, wg, wu, wd)


def per_device(tokens, cotangent, route, prob, w_gate, w_up, w_down):
    tok_rows, quarter = tokens.shape
    local_exp, units, width = w_gate.shape
    groups = lax.axis_size("expert")
    halves = lax.axis_size("half")
    experts = local_exp * groups
    total = groups * tok_rows
    f32 = jnp.float32
    me = lax.axis_index("expert")

    fast = (
        groups > 2 and groups & (groups - 1) == 0 and halves == 2 * 2
        and tok_rows == LANES and quarter % (2 * LANES) == 0
        and units % 16 == 0 and local_exp <= 8 and experts <= 2 * LANES and route.shape[1] <= 8
        and 2 * total * width * 2 + 12 * local_exp * units * width <= VMEM_BYTES // 2
    )
    if fast:
        flat = (local_exp * units, width)
        grad_tokens, grad_prob, *grads = fused(
            tokens, cotangent, route, prob, w_gate.reshape(flat), w_up.reshape(flat),
            w_down.reshape(flat), groups, halves, local_exp,
        )
        grads = [g.reshape(local_exp, units, width) for g in grads]
        return (grad_tokens, grad_prob.T, *grads)

    hit = route[:, :, None] == jnp.arange(experts, dtype=route.dtype)
    table = jnp.sum(jnp.where(hit, prob[:, :, None], 0).astype(f32), axis=1).astype(prob.dtype)
    mine = lax.all_to_all(
        table.reshape(tok_rows, groups, local_exp), "expert",
        split_axis=1, concat_axis=0, tiled=True,
    ).reshape(total, local_exp)
    x = gather_all(tokens, groups, halves)
    d = gather_all(cotangent, groups, halves)
    weight = jnp.repeat(mine.astype(f32), units, axis=1)

    wg = w_gate.reshape(local_exp * units, width)
    wu = w_up.reshape(local_exp * units, width)
    wd = w_down.reshape(local_exp * units, width)
    nt = (((1,), (1,)), ((), ()))
    tn = (((0,), (0,)), ((), ()))
    gate = lax.dot_general(x, wg, nt, preferred_element_type=f32)
    upval = lax.dot_general(x, wu, nt, preferred_element_type=f32)
    raw = lax.dot_general(d, wd, nt, preferred_element_type=f32)
    sig = jax.nn.sigmoid(gate)
    act = gate * sig
    hidden = act * upval
    score = jnp.sum((hidden * raw).reshape(total, local_exp, units), axis=2)
    dact = weight * raw
    hp = (weight * hidden).astype(jnp.bfloat16)
    dgate = (dact * upval * sig * (1.0 + gate * (1.0 - sig))).astype(jnp.bfloat16)
    dup = (dact * act).astype(jnp.bfloat16)
    part = lax.dot_general(
        jnp.concatenate([dgate, dup], axis=1), jnp.concatenate([wg, wu], axis=0),
        (((1,), (0,)), ((), ())), preferred_element_type=f32,
    ).astype(jnp.bfloat16)
    part = part.reshape(groups, tok_rows, halves, quarter).transpose(0, 2, 1, 3)
    grad_tokens = lax.psum_scatter(
        part.reshape(groups * halves * tok_rows, quarter), BOTH,
        scatter_dimension=0, tiled=True,
    )
    sent = jnp.broadcast_to(
        score.reshape(groups, 1, tok_rows, local_exp), (groups, halves, tok_rows, local_exp)
    ).reshape(groups * halves, tok_rows * local_exp)
    back = lax.all_to_all(sent, BOTH, split_axis=0, concat_axis=0, tiled=True)
    back = jnp.sum(back.reshape(groups, halves, tok_rows, local_exp), axis=1)
    back = back.transpose(1, 0, 2).reshape(tok_rows, 1, experts)
    grad_prob = jnp.sum(jnp.where(hit, back, 0), axis=2)
    shape = (local_exp, units, width)
    grad_gate = lax.dot_general(dgate, x, tn, preferred_element_type=f32).astype(jnp.bfloat16)
    grad_up = lax.dot_general(dup, x, tn, preferred_element_type=f32).astype(jnp.bfloat16)
    grad_down = lax.dot_general(hp, d, tn, preferred_element_type=f32).astype(jnp.bfloat16)
    return (
        grad_tokens,
        grad_prob,
        grad_gate.reshape(shape),
        grad_up.reshape(shape),
        grad_down.reshape(shape),
    )


def solution(mesh):
    in_specs = (
        P("expert", "half"),
        P("expert", "half"),
        P("expert", None),
        P("expert", None),
        P("expert", "half", None),
        P("expert", "half", None),
        P("expert", "half", None),
    )
    out_specs = (
        P("expert", "half"),
        P("expert", None),
        P("expert", "half", None),
        P("expert", "half", None),
        P("expert", "half", None),
    )
    return jax.shard_map(
        per_device, mesh=mesh, in_specs=in_specs, out_specs=out_specs, check_vma=False
    )
```

time: 131 us -> 92.1 us (0.70)
  matrix products: 26.9 us -> 0 us
  Pallas kernels: 94.6 us -> 83.2 us
  other arithmetic: 3.44 us -> 0 us
  local copies, waits for them, and re-layouts: 4.9 us -> 8.07 us
    dot_general x7 -> x0, matrix products: 26.9 us -> none  [the longest x1 5.51 us: per_device(): lax.dot_general(dgate, x, tn, preferred_element_type=f32)]
    pallas_call x2 -> x1, Pallas kernels: 94.6 us -> 83.2 us  [fused(): pl.pallas_call(functools.partial(fused_kernel, groups, halves, local_exp)...]
    unnamed x21 -> x11, local copies, waits for them, and re-layouts: 3.35 us -> 8.07 us
    reduce_sum x4 -> x0, other arithmetic: 2.35 us -> none  [the longest x1 0.92 us: per_device(): jnp.sum(back, axis=1).transpose(2, 0, 1).reshape(tok_rows, 1, experts)]
where the time goes in v1:
time: 92.1 us; the launch traced here: 91.9 us
  Pallas kernels  83.2 us (90%)
  local copies, waits for them, and re-layouts  8.07 us (9%)
    pallas_call x1, Pallas kernels, fused(): pl.pallas_call(functools.partial(fused_kernel, groups, halves, local_exp)...  83.2 us
    unnamed x11, local copies, waits for them, and re-layouts  8.07 us

profile of v1, /device:TPU:0, one launch (start us, length us, event | category | flops | bytes accessed | tf_op | source)
XLA Modules:
  0.0 91.9 jit_solution(17143521233808110000)
XLA Ops:
  0.6 0.8 copy.13.prob_ref
  1.4 0.8 copy.12.route_ref
  2.2 0.0 copy-start
  2.2 0.9 copy-done
  3.1 0.0 copy-start.1
  3.1 0.9 copy-done.1
  4.0 83.2 %shard_map.110 = (bf16[128,512]{1,0:T(8,128)(2,1)S(1)}, f32[8,128]{1,0:T(8,128)S(1)}, bf16[384,2048]{1,0:T(8,128)(2,1)S(1)}, bf16[384,2048]{1,0:T(8,128)(2,1)S(1)}, bf16[384,2048]{1,0:T(8,128)(2,1)S(1)}) custom-call(bf16[128,512]{1,0:T(8,128)(2,1)S(1)} %copy-done, bf16[128,512]{1,0:T(8,128)(2,1)S(1)} %copy-done.1, s32[128,8]{1,0:T(8,128)S(1)} %copy.12.route_ref, ...), custom_call_target="tpu_custom_call" | custom-call | tf_op jit(solution)/shard_map/pallas_call | solution.py:411
  87.2 0.7 copy.19
  87.9 0.6 copy.20
  88.5 1.1 %copy.21 = bf16[2,192,2048]{2,1,0:T(8,128)(2,1)} copy(bf16[2,192,2048]{2,1,0:T(8,128)(2,1)S(1)} %bitcast.9) | data formatting | bytes 3145728
  89.6 1.1 %copy.22 = bf16[2,192,2048]{2,1,0:T(8,128)(2,1)} copy(bf16[2,192,2048]{2,1,0:T(8,128)(2,1)S(1)} %bitcast.8) | data formatting | bytes 3145728
  90.7 1.1 %copy.23 = bf16[2,192,2048]{2,1,0:T(8,128)(2,1)} copy(bf16[2,192,2048]{2,1,0:T(8,128)(2,1)S(1)} %bitcast.7) | data formatting | bytes 3145728
Async XLA Ops:
  2.2 0.9 copy-start
  3.1 0.9 copy-start.1

commit v2 on v1

--- a/solution.py
+++ b/solution.py
@@ -18,6 +18,7 @@
 
 LANES = 128
 VMEM_BYTES = 48 << 20
+DRAIN_BYTES = 1 << 20
 MESH = pl.DeviceIdType.MESH
 
 
@@ -45,9 +46,9 @@
 def fused_kernel(
     groups, halves, local_exp, tok_ref, cot_ref, route_ref, prob_ref, wg_ref, wu_ref, wd_ref,
     gt_ref, gp_ref, gg_ref, gu_ref, gd_ref,
-    xb, db, wgu, wdn, gates, raws, dgu, hps, turned, tab_own, tab_in, score, back,
+    xb, db, wgu, wdn, gates, raws, dgu, hps, turned, route_in, prob_in, tab_own, tab_in, score, back,
     psend, own, cin, acc, xin0, yin0, yin1, xin1, t0, t1, fin, zin,
-    first_send, second_send, core_send, z_send, z_sem, p_sem, q_sem, c_sem, own_sem, w_sem,
+    first_send, second_send, core_send, rest_send, z_send, z_sem, p_sem, q_sem, c_sem, own_sem, w_sem,
     tab_send, tab_recv, score_send, score_recv,
     part_send, part_recv, hop_send, hop_recv, last_send, last_recv,
 ):
@@ -59,7 +60,7 @@
     hidden_rows, width = wg_ref.shape
     units = hidden_rows // local_exp
     experts = local_exp * groups
-    top = route_ref.shape[1]
+    top = route_ref.shape[0]
     f32, b16 = jnp.float32, tok_ref.dtype
     nt = (((1,), (1,)), ((), ()))
     nn = (((1,), (0,)), ((), ()))
@@ -67,14 +68,30 @@
     x_peer = (e, 2 * (1 - x) + c)
     c_peer = (e, 2 * x + 1 - c)
 
-    eye = (
-        lax.broadcasted_iota(jnp.int32, (top, top), 0)
-        == lax.broadcasted_iota(jnp.int32, (top, top), 1)
-    ).astype(f32)
-    flip = lambda a: lax.dot_general(eye, a, nt, preferred_element_type=f32)
-    route_t = flip(route_ref[...].astype(f32))
-    prob_t = flip(prob_ref[...].astype(f32))
-    row_of = lax.broadcasted_iota(jnp.int32, (experts, rows), 0).astype(f32)
+    def local(src, dst, sem):
+        copy = pltpu.make_async_copy(src, dst, sem)
+        copy.start()
+        return copy
+
+    def slot(out, s, yy, xx, cc):
+        row = pl.multiple_of((2 * s + yy) * rows, rows)
+        col = pl.multiple_of((2 * xx + cc) * quarter, quarter)
+        return out.at[pl.ds(row, rows), pl.ds(col, quarter)]
+
+    pair = ((tok_ref, xb), (cot_ref, db))
+
+    def at(a, s, kind, cc):
+        over = (kind % 2, kind // 2) if a == 0 else (kind // 2, kind % 2)
+        return slot(pair[a][1], s, 1 - y if over[0] else y, 1 - x if over[1] else x, cc)
+
+    mine = [local(pair[a][0], at(a, 0, 0, c), own_sem.at[1 + a]) for a in range(2)]
+
+    small = [local(route_ref, route_in, w_sem.at[3]), local(prob_ref, prob_in, w_sem.at[4])]
+    for copy in small:
+        copy.wait()
+    route_t = route_in[...]
+    prob_t = prob_in[...].astype(f32)
+    row_of = lax.broadcasted_iota(jnp.int32, (experts, rows), 0)
     table = jnp.zeros((experts, rows), f32)
     for k in range(top):
         table = table + jnp.where(row_of == route_t[k:k + 1, :], prob_t[k:k + 1, :], 0.0)
@@ -102,51 +119,49 @@
             device_id=c_peer, device_id_type=MESH,
         ).wait_recv()
 
-    def local(src, dst, sem):
-        copy = pltpu.make_async_copy(src, dst, sem)
-        copy.start()
-        return copy
-
-    def slot(out, s, yy, xx, cc):
-        row = pl.multiple_of((2 * s + yy) * rows, rows)
-        col = pl.multiple_of((2 * xx + cc) * quarter, quarter)
-        return out.at[pl.ds(row, rows), pl.ds(col, quarter)]
-
-    pair = ((tok_ref, xb), (cot_ref, db))
-
-    def at(a, s, kind, cc):
-        along = (kind % 2, kind // 2) if a == 0 else (kind // 2, kind % 2)
-        return slot(pair[a][1], s, 1 - y if along[0] else y, 1 - x if along[1] else x, cc)
-
     hops = ((y_peer, x_peer), (x_peer, y_peer))
 
     def gather_own(s):
-        have = []
-        for a in range(2):
-            there = at(a, s, 0, c)
+        have = [at(a, s, 0, c) for a in range(2)]
+        for a in range(2):
             if s > 0:
-                arrived(there, z_sem.at[a, s])
-            have.append((pair[a][0] if s == 0 else there, there))
-            push(*have[a], hops[a][0], first_send.at[a, s], p_sem.at[a, s])
-        for a in range(2):
-            push(*have[a], hops[a][1], second_send.at[a, s], q_sem.at[a, s])
-        for a in range(2):
-            push(*have[a], c_peer, core_send.at[a, s], c_sem.at[a, s])
+                arrived(have[a], z_sem.at[a, s])
+            if s != 1:
+                push(have[a], have[a], hops[a][0], first_send.at[a, s], p_sem.at[a, s])
+        for a in range(2):
+            push(have[a], have[a], hops[a][1], second_send.at[a, s], q_sem.at[a, s])
+        for a in range(2):
+            push(have[a], have[a], c_peer, core_send.at[a, s], c_sem.at[a, s])
 
     def gather_first(s):
-        for a in range(2):
-            there = at(a, s, 1, c)
-            arrived(there, p_sem.at[a, s])
-            push(there, there, hops[a][1], second_send.at[a, line + s], q_sem.at[a, line + s])
-        for a in range(2):
-            there = at(a, s, 1, c)
-            push(there, there, c_peer, core_send.at[a, line + s], c_sem.at[a, line + s])
+        there = [at(a, s, 1, c) for a in range(2)]
+        for a in range(2):
+            arrived(there[a], p_sem.at[a, s])
+            if s != 1:
+                push(
+                    there[a], there[a], hops[a][1],
+                    second_send.at[a, line + s], q_sem.at[a, line + s],
+                )
+        for a in range(2):
+            push(there[a], there[a], c_peer, core_send.at[a, line + s], c_sem.at[a, line + s])
 
     def gather_second(s, kind):
         for a in range(2):
             there = at(a, s, kind, c)
             arrived(there, q_sem.at[a, (kind - 2) * line + s])
             push(there, there, c_peer, core_send.at[a, kind * line + s], c_sem.at[a, kind * line + s])
+
+    def along(s):
+        return (2 * across(z, s) + y, h)
+
+    def send_plane(s):
+        for a in range(2):
+            push(at(a, 0, 0, c), at(a, s, 0, c), along(s), z_send.at[a, s], z_sem.at[a, s])
+
+    def send_rest(kind):
+        for a in range(2):
+            sem = p_sem.at[a, 1] if kind == 1 else q_sem.at[a, line + 1]
+            push(at(a, 0, kind, c), at(a, 1, kind, c), along(1), rest_send.at[a, kind // 2], sem)
 
     def gather_core(s):
         for a in range(2):
@@ -207,7 +222,6 @@
         copies = []
         for xx in range(2):
             psend[s, xx] = part_of(xx, 1 - c)
-        for xx in range(2):
             push(psend.at[s, xx], cin.at[s, xx], c_peer, part_send.at[s, xx], part_recv.at[s, xx])
         for xx in range(2):
             own[s, xx] = part_of(xx, c)
@@ -303,63 +317,89 @@
             hps[...], db[:, cols], nn, preferred_element_type=f32
         ).astype(b16)
 
+    for copy in mine:
+        copy.wait()
+    def send_table():
+        for s in range(line):
+            for dy in range(2):
+                if s + dy:
+                    push(
+                        tab_own, tab_in.at[s, dy], (2 * across(z, s) + flipped(dy), h),
+                        tab_send.at[s, dy], tab_recv.at[s, dy],
+                    )
+
+    def table_in(s):
+        for dy in range(2):
+            if s + dy:
+                arrived(tab_in.at[s, dy], tab_recv.at[s, dy])
+
+    def finish(s):
+        middle(s)
+        send_part(s)
+        send_score(s)
+
     gather_own(0)
-    for a in range(2):
-        for s in range(1, line):
-            push(
-                pair[a][0], slot(pair[a][1], s, y, x, c), (2 * across(z, s) + y, h),
-                z_send.at[a, s], z_sem.at[a, s],
-            )
+    send_plane(1)
+    send_plane(2)
+    send_table()
     weights = [
         local(wg_ref, wgu.at[pl.ds(0, hidden_rows)], w_sem.at[0]),
         local(wu_ref, wgu.at[pl.ds(hidden_rows, hidden_rows)], w_sem.at[1]),
         local(wd_ref, wdn, w_sem.at[2]),
     ]
-    mine = [local(pair[a][0], at(a, 0, 0, c), own_sem.at[1 + a]) for a in range(2)]
-    for s in range(line):
-        for dy in range(2):
-            if s + dy:
-                push(
-                    tab_own, tab_in.at[s, dy], (2 * across(z, s) + flipped(dy), h),
-                    tab_send.at[s, dy], tab_recv.at[s, dy],
-                )
     gather_first(0)
-    for copy in weights + mine:
+    gather_second(0, 2)
+    gather_own(1)
+    send_plane(3)
+    send_rest(1)
+    gather_second(0, 3)
+    send_rest(3)
+    gather_core(0)
+    for copy in weights:
         copy.wait()
-
-    for s in range(line):
-        if s + 1 < line:
-            gather_own(s + 1)
-        if s >= 1:
-            settle_core(s - 1)
-        gather_second(s, 2)
-        gather_second(s, 3)
-        gather_core(s)
-        for dy in range(2):
-            if s + dy:
-                arrived(tab_in.at[s, dy], tab_recv.at[s, dy])
-        if s >= 2:
-            settle_second(s - 2)
-        forward(s)
-        if s + 1 < line:
-            gather_first(s + 1)
-        if s >= 1:
-            settle_first(s - 1)
-        middle(s)
-        send_part(s)
-        send_score(s)
-
-    settle_core(line - 1)
-    settle_second(line - 2)
-    pieces = width // cut
-    halfway = pieces // 2
-    for n in range(halfway):
-        grads_in(n)
-    settle_first(line - 1)
-    for n in range(halfway, pieces):
-        grads_in(n)
-    settle_second(line - 1)
-    for n in range(pieces):
+    table_in(0)
+    forward(0)
+    gather_own(2)
+    finish(0)
+    gather_second(1, 2)
+    gather_first(2)
+    settle_core(0)
+    gather_second(2, 2)
+    gather_second(2, 3)
+    gather_core(2)
+    table_in(2)
+    forward(2)
+    gather_own(3)
+    finish(2)
+    settle_first(0)
+    gather_first(3)
+    settle_core(2)
+    gather_first(1)
+    gather_second(1, 3)
+    gather_core(1)
+    table_in(1)
+    forward(1)
+    finish(1)
+    settle_second(0)
+    gather_second(3, 2)
+    gather_second(3, 3)
+    gather_core(3)
+    settle_core(1)
+    table_in(3)
+    forward(3)
+    settle_first(2)
+    finish(3)
+    settle_second(2)
+    settle_first(1)
+    settle_core(3)
+    grads_in(0)
+    grads_in(1)
+    settle_second(1)
+    settle_first(3)
+    grads_in(2)
+    grads_in(3)
+    settle_second(3)
+    for n in range(width // cut):
         grads_out(n)
 
     for copy in owns:
@@ -380,7 +420,7 @@
             first = local_exp * (2 * across(z, s) + flipped(dy))
             for l in range(local_exp):
                 total = total + jnp.where(
-                    route_t == (first + l).astype(f32), block[l:l + 1, :], 0.0
+                    route_t == first + l, block[l:l + 1, :], 0.0
                 )
     gp_ref[...] = total
     for s in range(1, line):
@@ -401,11 +441,11 @@
     rows, quarter = tokens.shape
     line, wide = groups // 2, quarter // 2
     hidden_rows, width = wg.shape
-    experts, top = local_exp * groups, route.shape[1]
+    experts, top = local_exp * groups, route.shape[0]
     b16, f32 = tokens.dtype, jnp.float32
     dma = pltpu.SemaphoreType.DMA
     vmem = pl.BlockSpec(memory_space=pltpu.VMEM)
-    hbm = pl.BlockSpec(memory_space=pl.ANY)
+    hbm = pl.BlockSpec(memory_space=pltpu.HBM)
     total = groups * rows
     grad = jax.ShapeDtypeStruct((hidden_rows, width), b16)
     return pl.pallas_call(
@@ -415,7 +455,7 @@
             jax.ShapeDtypeStruct((top, rows), f32),
             grad, grad, grad,
         ),
-        in_specs=[vmem] * 4 + [hbm] * 3,
+        in_specs=[hbm] * 7,
         out_specs=[vmem] * 5,
         scratch_shapes=[
             pltpu.VMEM((total, width), b16),
@@ -427,6 +467,8 @@
             pltpu.VMEM((2 * hidden_rows, total), b16),
             pltpu.VMEM((hidden_rows, total), b16),
             pltpu.VMEM((2 * rows, 2 * hidden_rows), b16),
+            pltpu.VMEM(route.shape, route.dtype),
+            pltpu.VMEM(prob.shape, prob.dtype),
             pltpu.VMEM((experts, rows), f32),
             pltpu.VMEM((line, 2, experts, rows), f32),
             pltpu.VMEM((line, 2, 8, rows), f32),
@@ -443,9 +485,9 @@
             pltpu.VMEM((line, 2, rows, wide), b16),
             pltpu.VMEM((line, rows, quarter), b16),
             pltpu.VMEM((line, rows, quarter), b16),
-            dma((2, line)), dma((2, 2 * line)), dma((2, 4 * line)), dma((2, line)),
+            dma((2, line)), dma((2, 2 * line)), dma((2, 4 * line)), dma((2, 2)), dma((2, line)),
             dma((2, line)), dma((2, line)), dma((2, 2 * line)), dma((2, 4 * line)),
-            dma((4,)), dma((3,)),
+            dma((4,)), dma((5,)),
             dma((line, 2)), dma((line, 2)),
             dma((line, 2, halves)), dma((line, 2, halves)),
             dma((line, 2)), dma((line, 2)),
@@ -458,6 +500,27 @@
     )(tokens, cotangent, route, prob, wg, wu, wd)
 
 
+def drain_kernel(count, *refs):
+    sources, targets, sem = refs[:count], refs[count:2 * count], refs[2 * count]
+    copies = [pltpu.make_async_copy(a, b, sem.at[i]) for i, (a, b) in enumerate(zip(sources, targets))]
+    for copy in copies:
+        copy.start()
+    for copy in copies:
+        copy.wait()
+
+
+def drain(arrays):
+    count = len(arrays)
+    return pl.pallas_call(
+        functools.partial(drain_kernel, count),
+        out_shape=[jax.ShapeDtypeStruct(a.shape, a.dtype) for a in arrays],
+        in_specs=[pl.BlockSpec(memory_space=pltpu.VMEM)] * count,
+        out_specs=[pl.BlockSpec(memory_space=pl.ANY)] * count,
+        scratch_shapes=[pltpu.SemaphoreType.DMA((count,))],
+        compiler_params=pltpu.CompilerParams(vmem_limit_bytes=DRAIN_BYTES),
+    )(*arrays)
+
+
 def per_device(tokens, cotangent, route, prob, w_gate, w_up, w_down):
     tok_rows, quarter = tokens.shape
     local_exp, units, width = w_gate.shape
@@ -469,17 +532,18 @@
     me = lax.axis_index("expert")
 
     fast = (
-        groups > 2 and groups & (groups - 1) == 0 and halves == 2 * 2
+        groups == 2 * halves and halves == 2 * 2 and width == 4 * quarter
         and tok_rows == LANES and quarter % (2 * LANES) == 0
         and units % 16 == 0 and local_exp <= 8 and experts <= 2 * LANES and route.shape[1] <= 8
         and 2 * total * width * 2 + 12 * local_exp * units * width <= VMEM_BYTES // 2
     )
     if fast:
         flat = (local_exp * units, width)
-        grad_tokens, grad_prob, *grads = fused(
-            tokens, cotangent, route, prob, w_gate.reshape(flat), w_up.reshape(flat),
+        results = fused(
+            *[pltpu.with_memory_space_constraint(v, pltpu.HBM) for v in (tokens, cotangent, route.T, prob.T)], w_gate.reshape(flat), w_up.reshape(flat),
             w_down.reshape(flat), groups, halves, local_exp,
         )
+        grad_tokens, grad_prob, *grads = drain(results)
         grads = [g.reshape(local_exp, units, width) for g in grads]
         return (grad_tokens, grad_prob.T, *grads)
 

time: 92.1 us -> 78.7 us (0.85)
  local copies, waits for them, and re-layouts: 8.07 us -> 0 us
  Pallas kernels: 83.2 us -> 77.9 us
    unnamed x11 -> x0, local copies, waits for them, and re-layouts: 8.07 us -> none
    pallas_call x1, Pallas kernels: 83.2 us -> 75.6 us  [fused(): pl.pallas_call(functools.partial(fused_kernel, groups, halves, local_exp)...]
    pallas_call x0 -> x1, Pallas kernels: none -> 2.27 us  [drain(): pl.pallas_call(functools.partial(drain_kernel, count), out_shape=[jax.Sha...]
where the time goes in v2:
time: 78.7 us; the launch traced here: 78.5 us
  Pallas kernels  77.9 us (99%)
    pallas_call x1, Pallas kernels, fused(): pl.pallas_call(functools.partial(fused_kernel, groups, halves, local_exp)...  75.6 us
    pallas_call x1, Pallas kernels, drain(): pl.pallas_call(functools.partial(drain_kernel, count), out_shape=[jax.Sha...  2.27 us

profile of v2, /device:TPU:0, one launch (start us, length us, event | category | flops | bytes accessed | tf_op | source)
XLA Modules:
  0.0 78.5 jit_solution(6975730244098339385)
XLA Ops:
  0.6 75.6 %shard_map.110 = (bf16[128,512]{1,0:T(8,128)(2,1)S(1)}, f32[8,128]{1,0:T(8,128)S(1)}, bf16[384,2048]{1,0:T(8,128)(2,1)S(1)}, bf16[384,2048]{1,0:T(8,128)(2,1)S(1)}, bf16[384,2048]{1,0:T(8,128)(2,1)S(1)}) custom-call(bf16[128,512]{1,0:T(8,128)(2,1)} %tok_ref.1, bf16[128,512]{1,0:T(8,128)(2,1)} %cot_ref.1, s32[8,128]{1,0:T(8,128)} %bitcast.12, ...), custom_call_target="tpu_custom_call" | custom-call | tf_op jit(solution)/shard_map/pallas_call | solution.py:451
  76.3 2.3 %shard_map.111 = (bf16[128,512]{1,0:T(8,128)(2,1)}, f32[8,128]{1,0:T(8,128)}, bf16[384,2048]{1,0:T(8,128)(2,1)}, bf16[384,2048]{1,0:T(8,128)(2,1)}, bf16[384,2048]{1,0:T(8,128)(2,1)}) custom-call(bf16[128,512]{1,0:T(8,128)(2,1)S(1)} %get-tuple-element.15.refs_0_, f32[8,128]{1,0:T(8,128)S(1)} %get-tuple-element.16.refs_1_, ...), custom_call_target="tpu_custom_call" | custom-call | tf_op jit(solution)/shard_map/pallas_call | solution.py:514

commit v3 on v2

--- a/solution.py
+++ b/solution.py
@@ -46,9 +46,9 @@
 def fused_kernel(
     groups, halves, local_exp, tok_ref, cot_ref, route_ref, prob_ref, wg_ref, wu_ref, wd_ref,
     gt_ref, gp_ref, gg_ref, gu_ref, gd_ref,
-    xb, db, wgu, wdn, gates, raws, dgu, hps, turned, route_in, prob_in, tab_own, tab_in, score, back,
+    xb, db, wgu, wsides, wdn, gates, raws, dgu, hps, turned, route_in, prob_in, tab_own, tab_in, score, back,
     psend, own, cin, acc, xin0, yin0, yin1, xin1, t0, t1, fin, zin,
-    first_send, second_send, core_send, rest_send, z_send, z_sem, p_sem, q_sem, c_sem, own_sem, w_sem,
+    first_send, second_send, core_send, rest_send, pass_send, z_send, z_sem, p_sem, q_sem, c_sem, own_sem, w_sem,
     tab_send, tab_recv, score_send, score_recv,
     part_send, part_recv, hop_send, hop_recv, last_send, last_recv,
 ):
@@ -121,15 +121,61 @@
 
     hops = ((y_peer, x_peer), (x_peer, y_peer))
 
+    def along(s):
+        return (2 * across(z, s) + y, h)
+
+    middle_chip = lax.div(z + 1, 2) == 1
+    passed = []
+
+    def pass_on(src, s_to, step, a, number):
+        copy = pltpu.make_async_remote_copy(
+            src_ref=src, dst_ref=at(a, s_to, 0, c), send_sem=pass_send.at[a, number],
+            recv_sem=z_sem.at[a, s_to], device_id=along(step), device_id_type=MESH,
+        )
+        passed.append(copy)
+        return copy
+
+    def start_middle():
+        copies = [pass_on(at(a, 0, 0, c), 3, 3, a, 0) for a in range(2)]
+
+        @pl.when(middle_chip)
+        def _():
+            for copy in copies:
+                copy.start()
+
+    def relay_near():
+        inner = [pass_on(at(a, 1, 0, c), 2, 3, a, 1) for a in range(2)]
+        outer = [pass_on(at(a, 3, 0, c), 2, 1, a, 2) for a in range(2)]
+
+        @pl.when(middle_chip)
+        def _():
+            for a in range(2):
+                arrived(at(a, 1, 0, c), z_sem.at[a, 1])
+                inner[a].start()
+                arrived(at(a, 3, 0, c), z_sem.at[a, 3])
+                outer[a].start()
+
     def gather_own(s):
         have = [at(a, s, 0, c) for a in range(2)]
-        for a in range(2):
-            if s > 0:
+        far = [pass_on(at(a, 2, 0, c), 3, 1, a, 3) for a in range(2)] if s == 2 else None
+        for a in range(2):
+            if s == 2:
                 arrived(have[a], z_sem.at[a, s])
+
+                @pl.when(middle_chip)
+                def _():
+                    far[a].start()
+            elif s > 0:
+                @pl.when(jnp.logical_not(middle_chip))
+                def _():
+                    arrived(have[a], z_sem.at[a, s])
             if s != 1:
                 push(have[a], have[a], hops[a][0], first_send.at[a, s], p_sem.at[a, s])
-        for a in range(2):
-            push(have[a], have[a], hops[a][1], second_send.at[a, s], q_sem.at[a, s])
+            if s > 0:
+                push(have[a], have[a], hops[a][1], second_send.at[a, s], q_sem.at[a, s])
+        for a in range(2):
+            if s == 0:
+                push(have[a], have[a], hops[a][1], second_send.at[a, s], q_sem.at[a, s])
         for a in range(2):
             push(have[a], have[a], c_peer, core_send.at[a, s], c_sem.at[a, s])
 
@@ -151,9 +197,6 @@
             arrived(there, q_sem.at[a, (kind - 2) * line + s])
             push(there, there, c_peer, core_send.at[a, kind * line + s], c_sem.at[a, kind * line + s])
 
-    def along(s):
-        return (2 * across(z, s) + y, h)
-
     def send_plane(s):
         for a in range(2):
             push(at(a, 0, 0, c), at(a, s, 0, c), along(s), z_send.at[a, s], z_sem.at[a, s])
@@ -172,10 +215,18 @@
         return pl.ds(2 * s * rows, 2 * rows)
 
     def forward(s):
-        gates[...] = lax.dot_general(wgu[...], xb[plane(s), :], nt, preferred_element_type=f32)
+        for r in range(2):
+            part = pl.ds(r * hidden_rows, hidden_rows)
+            gates[part, :] = lax.dot_general(
+                wgu[part, :], xb[plane(s), :], nt, preferred_element_type=f32
+            )
 
     def middle(s):
-        raws[...] = lax.dot_general(wdn[...], db[plane(s), :], nt, preferred_element_type=f32)
+        for r in range(2):
+            part = pl.ds(r * hidden_rows // 2, hidden_rows // 2)
+            raws[part, :] = lax.dot_general(
+                wdn[part, :], db[plane(s), :], nt, preferred_element_type=f32
+            )
         chunk = 32 if units % 32 == 0 else 16
         expert_of = lax.broadcasted_iota(jnp.int32, (experts, rows), 0)
         lane = pl.ds(2 * s * rows, 2 * rows)
@@ -214,17 +265,20 @@
             score[s, yy] = block
         turned[...] = dgu[:, lane].T
 
-    def part_of(xx, cc):
-        cols = pl.ds(pl.multiple_of((2 * xx + cc) * quarter, quarter), quarter)
-        return lax.dot_general(turned[...], wgu[:, cols], nn, preferred_element_type=f32).astype(b16)
+    def part_of(side):
+        cols = pl.ds(side * 2 * quarter, 2 * quarter)
+        return lax.dot_general(
+            turned[...], wsides[:, cols], nn, preferred_element_type=f32
+        ).astype(b16)
 
     def send_part(s):
-        copies = []
+        theirs = part_of(0)
         for xx in range(2):
-            psend[s, xx] = part_of(xx, 1 - c)
+            psend[s, xx] = theirs[:, xx * quarter:(xx + 1) * quarter]
             push(psend.at[s, xx], cin.at[s, xx], c_peer, part_send.at[s, xx], part_recv.at[s, xx])
+        mine = part_of(1)
         for xx in range(2):
-            own[s, xx] = part_of(xx, c)
+            own[s, xx] = mine[:, xx * quarter:(xx + 1) * quarter]
 
     def flipped(dy):
         return 1 - y if dy else y
@@ -340,67 +394,81 @@
 
     gather_own(0)
     send_plane(1)
-    send_plane(2)
+    start_middle()
     send_table()
     weights = [
         local(wg_ref, wgu.at[pl.ds(0, hidden_rows)], w_sem.at[0]),
         local(wu_ref, wgu.at[pl.ds(hidden_rows, hidden_rows)], w_sem.at[1]),
         local(wd_ref, wdn, w_sem.at[2]),
     ]
+    for r, ref in enumerate((wg_ref, wu_ref)):
+        for n in range(4):
+            q = 2 * (n % 2) + (c if n // 2 else 1 - c)
+            weights.append(local(
+                ref.at[:, pl.ds(pl.multiple_of(q * quarter, quarter), quarter)],
+                wsides.at[pl.ds(r * hidden_rows, hidden_rows), pl.ds(n * quarter, quarter)],
+                w_sem.at[5 + 4 * r + n],
+            ))
     gather_first(0)
+    relay_near()
+    gather_own(1)
     gather_second(0, 2)
-    gather_own(1)
-    send_plane(3)
+    gather_second(0, 3)
+    gather_core(0)
+    gather_own(2)
     send_rest(1)
-    gather_second(0, 3)
     send_rest(3)
-    gather_core(0)
     for copy in weights:
         copy.wait()
     table_in(0)
     forward(0)
-    gather_own(2)
+    gather_second(1, 2)
     finish(0)
-    gather_second(1, 2)
     gather_first(2)
+    gather_own(3)
     settle_core(0)
     gather_second(2, 2)
     gather_second(2, 3)
     gather_core(2)
     table_in(2)
     forward(2)
-    gather_own(3)
+    gather_first(3)
     finish(2)
     settle_first(0)
-    gather_first(3)
+    gather_first(1)
     settle_core(2)
-    gather_first(1)
+    gather_second(3, 2)
+    gather_second(3, 3)
     gather_second(1, 3)
+    gather_core(3)
+    table_in(3)
+    forward(3)
+    settle_second(0)
+    middle(3)
+    send_part(3)
+    settle_first(2)
     gather_core(1)
     table_in(1)
     forward(1)
-    finish(1)
-    settle_second(0)
-    gather_second(3, 2)
-    gather_second(3, 3)
-    gather_core(3)
+    settle_core(3)
+    middle(1)
+    send_part(1)
+    settle_second(2)
+    settle_first(3)
     settle_core(1)
-    table_in(3)
-    forward(3)
-    settle_first(2)
-    finish(3)
-    settle_second(2)
-    settle_first(1)
-    settle_core(3)
+    send_score(3)
+    send_score(1)
     grads_in(0)
     grads_in(1)
-    settle_second(1)
-    settle_first(3)
+    settle_second(3)
     grads_in(2)
     grads_in(3)
-    settle_second(3)
-    for n in range(width // cut):
-        grads_out(n)
+    settle_first(1)
+    grads_out(0)
+    grads_out(1)
+    settle_second(1)
+    grads_out(2)
+    grads_out(3)
 
     for copy in owns:
         copy.wait()
@@ -436,6 +504,11 @@
     for copy in sends:
         copy.wait_send()
 
+    @pl.when(middle_chip)
+    def _():
+        for copy in passed:
+            copy.wait_send()
+
 
 def fused(tokens, cotangent, route, prob, wg, wu, wd, groups, halves, local_exp):
     rows, quarter = tokens.shape
@@ -460,6 +533,7 @@
         scratch_shapes=[
             pltpu.VMEM((total, width), b16),
             pltpu.VMEM((total, width), b16),
+            pltpu.VMEM((2 * hidden_rows, width), b16),
             pltpu.VMEM((2 * hidden_rows, width), b16),
             pltpu.VMEM((hidden_rows, width), b16),
             pltpu.VMEM((2 * hidden_rows, 2 * rows), f32),
@@ -485,9 +559,9 @@
             pltpu.VMEM((line, 2, rows, wide), b16),
             pltpu.VMEM((line, rows, quarter), b16),
             pltpu.VMEM((line, rows, quarter), b16),
-            dma((2, line)), dma((2, 2 * line)), dma((2, 4 * line)), dma((2, 2)), dma((2, line)),
+            dma((2, line)), dma((2, 2 * line)), dma((2, 4 * line)), dma((2, 2)), dma((2, 4)), dma((2, line)),
             dma((2, line)), dma((2, line)), dma((2, 2 * line)), dma((2, 4 * line)),
-            dma((4,)), dma((5,)),
+            dma((4,)), dma((13,)),
             dma((line, 2)), dma((line, 2)),
             dma((line, 2, halves)), dma((line, 2, halves)),
             dma((line, 2)), dma((line, 2)),
@@ -534,7 +608,7 @@
     fast = (
         groups == 2 * halves and halves == 2 * 2 and width == 4 * quarter
         and tok_rows == LANES and quarter % (2 * LANES) == 0
-        and units % 16 == 0 and local_exp <= 8 and experts <= 2 * LANES and route.shape[1] <= 8
+        and units % 32 == 0 and local_exp <= 8 and experts <= 2 * LANES and route.shape[1] <= 8
         and 2 * total * width * 2 + 12 * local_exp * units * width <= VMEM_BYTES // 2
     )
     if fast:

time: 78.7 us -> 74.6 us (0.948)
  Pallas kernels: 77.9 us -> 73.7 us
    pallas_call x1, Pallas kernels: 75.6 us -> 71.5 us  [fused(): pl.pallas_call(functools.partial(fused_kernel, groups, halves, local_exp)...]
where the time goes in v3:
time: 74.6 us; the launch traced here: 74.4 us
  Pallas kernels  73.7 us (99%)
    pallas_call x1, Pallas kernels, fused(): pl.pallas_call(functools.partial(fused_kernel, groups, halves, local_exp)...  71.5 us
    pallas_call x1, Pallas kernels, drain(): pl.pallas_call(functools.partial(drain_kernel, count), out_shape=[jax.Sha...  2.27 us

profile of v3, /device:TPU:0, one launch (start us, length us, event | category | flops | bytes accessed | tf_op | source)
XLA Modules:
  0.0 74.4 jit_solution(12440361359140607619)
XLA Ops:
  0.6 71.5 %shard_map.110 = (bf16[128,512]{1,0:T(8,128)(2,1)S(1)}, f32[8,128]{1,0:T(8,128)S(1)}, bf16[384,2048]{1,0:T(8,128)(2,1)S(1)}, bf16[384,2048]{1,0:T(8,128)(2,1)S(1)}, bf16[384,2048]{1,0:T(8,128)(2,1)S(1)}) custom-call(bf16[128,512]{1,0:T(8,128)(2,1)} %tok_ref.1, bf16[128,512]{1,0:T(8,128)(2,1)} %cot_ref.1, s32[8,128]{1,0:T(8,128)} %bitcast.12, ...), custom_call_target="tpu_custom_call" | custom-call | tf_op jit(solution)/shard_map/pallas_call | solution.py:524
  72.1 2.3 %shard_map.111 = (bf16[128,512]{1,0:T(8,128)(2,1)}, f32[8,128]{1,0:T(8,128)}, bf16[384,2048]{1,0:T(8,128)(2,1)}, bf16[384,2048]{1,0:T(8,128)(2,1)}, bf16[384,2048]{1,0:T(8,128)(2,1)}) custom-call(bf16[128,512]{1,0:T(8,128)(2,1)S(1)} %get-tuple-element.15.refs_0_, f32[8,128]{1,0:T(8,128)S(1)} %get-tuple-element.16.refs_1_, ...), custom_call_target="tpu_custom_call" | custom-call | tf_op jit(solution)/shard_map/pallas_call | solution.py:588

commit v4 on v3

--- a/solution.py
+++ b/solution.py
@@ -434,39 +434,39 @@
     forward(2)
     gather_first(3)
     finish(2)
-    settle_first(0)
     gather_first(1)
     settle_core(2)
+    gather_second(1, 3)
+    gather_core(1)
+    table_in(1)
+    settle_first(0)
+    forward(1)
     gather_second(3, 2)
+    middle(1)
+    send_part(1)
     gather_second(3, 3)
-    gather_second(1, 3)
+    settle_core(1)
     gather_core(3)
     table_in(3)
     forward(3)
-    settle_second(0)
+    settle_first(2)
     middle(3)
     send_part(3)
-    settle_first(2)
-    gather_core(1)
-    table_in(1)
-    forward(1)
+    settle_second(0)
     settle_core(3)
-    middle(1)
-    send_part(1)
     settle_second(2)
-    settle_first(3)
-    settle_core(1)
+    settle_first(1)
+    send_score(1)
     send_score(3)
-    send_score(1)
     grads_in(0)
     grads_in(1)
+    settle_first(3)
+    grads_in(2)
+    settle_second(1)
+    grads_out(0)
     settle_second(3)
-    grads_in(2)
     grads_in(3)
-    settle_first(1)
-    grads_out(0)
     grads_out(1)
-    settle_second(1)
     grads_out(2)
     grads_out(3)
 

time: 74.6 us -> 71.8 us (0.962)
  Pallas kernels: 73.7 us -> 71 us
    pallas_call x1, Pallas kernels: 71.5 us -> 68.7 us  [fused(): pl.pallas_call(functools.partial(fused_kernel, groups, halves, local_exp)...]
where the time goes in v4:
time: 71.8 us; the launch traced here: 71.6 us
  Pallas kernels  71 us (99%)
    pallas_call x1, Pallas kernels, fused(): pl.pallas_call(functools.partial(fused_kernel, groups, halves, local_exp)...  68.7 us
    pallas_call x1, Pallas kernels, drain(): pl.pallas_call(functools.partial(drain_kernel, count), out_shape=[jax.Sha...  2.27 us

profile of v4, /device:TPU:0, one launch (start us, length us, event | category | flops | bytes accessed | tf_op | source)
XLA Modules:
  0.0 71.6 jit_solution(785842979677468827)
XLA Ops:
  0.6 68.7 %shard_map.110 = (bf16[128,512]{1,0:T(8,128)(2,1)S(1)}, f32[8,128]{1,0:T(8,128)S(1)}, bf16[384,2048]{1,0:T(8,128)(2,1)S(1)}, bf16[384,2048]{1,0:T(8,128)(2,1)S(1)}, bf16[384,2048]{1,0:T(8,128)(2,1)S(1)}) custom-call(bf16[128,512]{1,0:T(8,128)(2,1)} %tok_ref.1, bf16[128,512]{1,0:T(8,128)(2,1)} %cot_ref.1, s32[8,128]{1,0:T(8,128)} %bitcast.12, ...), custom_call_target="tpu_custom_call" | custom-call | tf_op jit(solution)/shard_map/pallas_call | solution.py:524
  69.4 2.3 %shard_map.111 = (bf16[128,512]{1,0:T(8,128)(2,1)}, f32[8,128]{1,0:T(8,128)}, bf16[384,2048]{1,0:T(8,128)(2,1)}, bf16[384,2048]{1,0:T(8,128)(2,1)}, bf16[384,2048]{1,0:T(8,128)(2,1)}) custom-call(bf16[128,512]{1,0:T(8,128)(2,1)S(1)} %get-tuple-element.15.refs_0_, f32[8,128]{1,0:T(8,128)S(1)} %get-tuple-element.16.refs_1_, ...), custom_call_target="tpu_custom_call" | custom-call | tf_op jit(solution)/shard_map/pallas_call | solution.py:588

commit v5 on v4

--- a/solution.py
+++ b/solution.py
@@ -426,7 +426,6 @@
     finish(0)
     gather_first(2)
     gather_own(3)
-    settle_core(0)
     gather_second(2, 2)
     gather_second(2, 3)
     gather_core(2)
@@ -436,10 +435,10 @@
     finish(2)
     gather_first(1)
     settle_core(2)
+    settle_core(0)
     gather_second(1, 3)
     gather_core(1)
     table_in(1)
-    settle_first(0)
     forward(1)
     gather_second(3, 2)
     middle(1)
@@ -451,8 +450,8 @@
     forward(3)
     settle_first(2)
     middle(3)
+    settle_first(0)
     send_part(3)
-    settle_second(0)
     settle_core(3)
     settle_second(2)
     settle_first(1)
@@ -469,6 +468,7 @@
     grads_out(1)
     grads_out(2)
     grads_out(3)
+    settle_second(0)
 
     for copy in owns:
         copy.wait()

time: 71.8 us -> 71.7 us (level)
  no operation moved by 1% of the time
where the time goes in v5:
time: 71.7 us; the launch traced here: 71.5 us
  Pallas kernels  70.8 us (99%)
    pallas_call x1, Pallas kernels, fused(): pl.pallas_call(functools.partial(fused_kernel, groups, halves, local_exp)...  68.6 us
    pallas_call x1, Pallas kernels, drain(): pl.pallas_call(functools.partial(drain_kernel, count), out_shape=[jax.Sha...  2.27 us

profile of v5, /device:TPU:0, one launch (start us, length us, event | category | flops | bytes accessed | tf_op | source)
XLA Modules:
  0.0 71.5 jit_solution(12104158436842189205)
XLA Ops:
  0.6 68.6 %shard_map.110 = (bf16[128,512]{1,0:T(8,128)(2,1)S(1)}, f32[8,128]{1,0:T(8,128)S(1)}, bf16[384,2048]{1,0:T(8,128)(2,1)S(1)}, bf16[384,2048]{1,0:T(8,128)(2,1)S(1)}, bf16[384,2048]{1,0:T(8,128)(2,1)S(1)}) custom-call(bf16[128,512]{1,0:T(8,128)(2,1)} %tok_ref.1, bf16[128,512]{1,0:T(8,128)(2,1)} %cot_ref.1, s32[8,128]{1,0:T(8,128)} %bitcast.12, ...), custom_call_target="tpu_custom_call" | custom-call | tf_op jit(solution)/shard_map/pallas_call | solution.py:524
  69.2 2.3 %shard_map.111 = (bf16[128,512]{1,0:T(8,128)(2,1)}, f32[8,128]{1,0:T(8,128)}, bf16[384,2048]{1,0:T(8,128)(2,1)}, bf16[384,2048]{1,0:T(8,128)(2,1)}, bf16[384,2048]{1,0:T(8,128)(2,1)}) custom-call(bf16[128,512]{1,0:T(8,128)(2,1)S(1)} %get-tuple-element.15.refs_0_, f32[8,128]{1,0:T(8,128)S(1)} %get-tuple-element.16.refs_1_, ...), custom_call_target="tpu_custom_call" | custom-call | tf_op jit(solution)/shard_map/pallas_call | solution.py:588
